TPU v7x, 512 devices: a whole 4x4x16 slice. The times are simulated.
512 devices in a mesh: vrow: 32 (over z_hi, x, y), aux: 8 (over z_lo), grp: 2 (over core).
Axes of the slice: x: 4, y: 4, z: 16 (z_hi: 2, z_lo: 8; z = z_hi * 8 + z_lo), core: 2. Of those that a mesh axis runs over, the one named last changes fastest.
Arguments:
- trials: bfloat16 [192, 3840], P(None, 'vrow'), may hold values from -6 to 6
- vv_factors: bfloat16 [64, 3840, 3840], P(('aux', 'grp'), 'vrow'), may hold values from -0.09375 to 0.09375
- screened: bfloat16 [64, 96, 96], P(('aux', 'grp')), may hold values from -0.078125 to 0.078125
- ov_factors: bfloat16 [64, 3840, 96], P(('aux', 'grp'), 'vrow'), may hold values from -0.0625 to 0.0625
- occ_energy: float32 [96], replicated, may hold values from -1.5 to -0.3
- virt_energy: float32 [3840], replicated, may hold values from 0.2 to 2.5
- occ_order: int32 [96], replicated, may hold values from 0 to 95, each once
- virt_order: int32 [3840], P('vrow'), may hold values from 0 to 3839, each once
Outputs:
- sigma: float32 [192, 3840], P(('aux', 'grp'), 'vrow')
Inputs may be any that keep to these rules, and one draw needn't show every extreme that they name: `occ_order`: each active occupied orbital names a different entry. `virt_order`: each virtual orbital names a different entry.
All inputs are finite; a program needn't handle non-finite values.
Results may differ from a plain program's by a relative error of at most 0.0022.
Values may be sent and summed in bfloat16 or wider, within the bound.
No kernel may reach another device: no remote copies, remote signals or barrier semaphores. Data moves between devices by JAX's collectives and lax.ppermute only.
A program may use at most 64 MiB of HBM per device.

v0:
```python
import jax
import jax.numpy as jnp
from jax import lax
from jax.experimental import pallas as pl
from jax.experimental.pallas import tpu as pltpu
from jax.sharding import Mesh
from jax.sharding import PartitionSpec as P

VROW = ("half", "x", "y")
PLANE = ("x", "y")
WINDOW = ("aux", "grp")
LANES = 128
ROWS = 128
PIECES = 3


def vmem():
    return pl.BlockSpec(memory_space=pltpu.VMEM)


def hbm():
    return pl.BlockSpec(memory_space=pltpu.HBM)


def in_pieces(values):
    pieces = []
    for _ in range(PIECES):
        piece = values.astype(jnp.bfloat16).astype(jnp.float32)
        pieces.append(piece)
        values = values - piece
    return pieces


def window_order(count):
    chips = count // 2
    middle = sorted(range(chips), key=lambda a: abs(2 * a + 1 - chips))
    listed = []
    for k in range(0, chips, 2):
        pair = middle[k : k + 2]
        listed += [2 * a + 1 for a in pair] + [2 * a for a in pair]
    return listed


def plane_order(count):
    first = 2 * count // 3
    return [first, *(place for place in range(count) if place != first)]


def pack_kernel(trials_hbm, ov_hbm, screened_hbm, block_ref, ov_ref, screened_ref, trials_ref, sems):
    copies = [
        pltpu.make_async_copy(trials_hbm, trials_ref, sems.at[0]),
        pltpu.make_async_copy(ov_hbm, ov_ref, sems.at[1]),
        pltpu.make_async_copy(screened_hbm, screened_ref, sems.at[2]),
    ]
    for copy in copies:
        copy.start()
    for copy in copies[:2]:
        copy.wait()
    core = lax.axis_index("grp")
    row = (lax.axis_index("half") * lax.axis_size("x") + lax.axis_index("x")) * lax.axis_size("y") + lax.axis_index("y")
    functions, occupied, virt = ov_ref.shape
    count = trials_ref.shape[0] // occupied
    spare = LANES - virt
    split = [trials_ref[pl.ds(t * occupied, occupied), :].astype(jnp.float32) for t in range(count)]
    factors = [ov_ref[q].astype(jnp.float32) for q in range(functions)]
    sums = [jnp.sum(factors[q] * split[t], axis=0, keepdims=True) for t in range(count) for q in range(functions)]
    sums = jnp.sum(jnp.concatenate(sums, axis=0), axis=1, keepdims=True)
    carried = PIECES * sums.shape[0]
    column = jnp.concatenate([*in_pieces(sums), jnp.zeros((occupied - carried, 1), jnp.float32)], axis=0)
    own = jnp.where(core == 0, split[0], split[1])
    wide = jnp.concatenate([own, jnp.broadcast_to(column, (occupied, spare))], axis=1)
    turn = lax.rem(row * virt, LANES)
    block_ref[...] = pltpu.roll(wide, turn, 1).astype(jnp.bfloat16)
    copies[2].wait()


def term_kernel(
    plane, window, both_ref, vv_hbm, vv_peer_hbm, screened_ref, screened_peer_ref, ov_ref, out_ref, whole_ref, held_ref, sems
):
    core = lax.axis_index("grp")
    half = lax.axis_index("half")
    functions, occupied, virt = ov_ref.shape
    copies = [
        [
            pltpu.make_async_copy(
                source.at[q],
                held_ref.at[pl.ds((side * functions + q) * ROWS, virt), :],
                sems.at[side * functions + q],
            )
            for q in range(functions)
        ]
        for side, source in enumerate((vv_hbm, vv_peer_hbm))
    ]
    for side in copies:
        for copy in side:
            copy.start()

    blocks = both_ref.shape[0]
    spare = LANES - virt
    tiles = blocks * virt // LANES
    entries = out_ref.shape[0] * out_ref.shape[1] // occupied * functions
    lanes = lax.broadcasted_iota(jnp.int32, (occupied, LANES), 1)
    few = lax.broadcasted_iota(jnp.int32, (PIECES * entries, LANES), 1)
    gathered = jnp.zeros((PIECES * entries, LANES), jnp.float32)
    for side in range(2):
        start = jnp.where(half == side, 0, tiles * LANES)
        held = both_ref[plane.index(0), side].astype(jnp.float32)
        for j in range(blocks):
            free = virt - spare * j
            picked = (few >= free) & (few < free + spare)
            gathered = gathered + jnp.where(picked, held[: PIECES * entries], 0.0)
            if j < tiles:
                after = both_ref[plane.index(j + 1), side].astype(jnp.float32)
                tile = jnp.where(lanes < free, held, after).astype(jnp.bfloat16)
                whole_ref[:, pl.ds(pl.multiple_of(start + j * LANES, LANES), LANES)] = tile
                held = after
    pair = jnp.sum(gathered, axis=1, keepdims=True) * (2.0 / spare)
    pair = sum(pair[k * entries : (k + 1) * entries] for k in range(PIECES))

    mine = jnp.zeros((occupied, virt), jnp.float32)
    other = jnp.zeros((occupied, virt), jnp.float32)
    for q in range(functions):
        factors = ov_ref[q].astype(jnp.float32)
        first, second = pair[q : q + 1], pair[functions + q : functions + q + 1]
        mine = mine + factors * jnp.where(core == 0, first, second)
        other = other + factors * jnp.where(core == 0, second, first)

    turned = jnp.zeros((virt, occupied), jnp.float32)
    for side, screen in enumerate((screened_ref, screened_peer_ref)):
        for copy in copies[side]:
            copy.wait()
        factor = held_ref[pl.ds(side * functions * ROWS, functions * ROWS), :]
        image = lax.dot_general(factor, whole_ref[...], (((1,), (1,)), ((), ())), preferred_element_type=jnp.float32)
        image = image.astype(jnp.bfloat16)
        for q in range(functions):
            turned = turned + jnp.dot(
                image[q * ROWS : q * ROWS + virt], screen[q], preferred_element_type=jnp.float32
            )
    mine = mine - turned.T

    share = out_ref.shape[1]
    per = occupied // share
    places = [window.index(w) for w in range(len(window))]
    for m in range(per):
        low, high = places[m], places[per + m]
        rows = slice(m * share, (m + 1) * share)
        out_ref[jnp.where(core == 0, low, high)] = mine[rows].astype(out_ref.dtype)
        out_ref[jnp.where(core == 0, high, low)] = other[rows].astype(out_ref.dtype)


def finish_kernel(terms_ref, base_ref, out_ref):
    total = base_ref[...]
    for place in range(terms_ref.shape[0]):
        total = total + terms_ref[place].astype(jnp.float32)
    out_ref[...] = total


def table_lookup(order, table):
    columns = lax.broadcasted_iota(jnp.int32, (order.shape[0], table.shape[0]), 1)
    picker = (order[:, None] == columns).astype(jnp.float32)
    return jnp.dot(picker, table, precision=lax.Precision.HIGHEST)


def level_part(trials, occ_energy, virt_energy, occ_order, virt_order, row_offset, row_share):
    occupied = occ_energy.shape[0]
    virt_levels = table_lookup(virt_order, virt_energy)
    occ_levels = table_lookup(occ_order, occ_energy)
    row_ids = row_offset + lax.broadcasted_iota(jnp.int32, (row_share,), 0)
    row_levels = table_lookup(row_ids % occupied, occ_levels)
    own_trials = lax.dynamic_slice_in_dim(trials, row_offset, row_share, 0).astype(jnp.float32)
    return (virt_levels[None, :] - row_levels[:, None]) * own_trials


def on_device(trials, vv_factors, screened, ov_factors, occ_energy, virt_energy, occ_order, virt_order):
    groups = lax.axis_size(WINDOW)
    rows_all, virt = trials.shape
    occupied = occ_energy.shape[0]
    functions, _, virt_all = vv_factors.shape
    row_share = rows_all // groups
    row_offset = lax.axis_index(WINDOW) * row_share
    ov_rows = jnp.swapaxes(ov_factors, 1, 2)
    peers = lax.axis_size(PLANE)
    window = window_order(groups)
    plane = plane_order(peers)
    cores = [(0, 1), (1, 0)]

    block, ov_held, screened_held = pl.pallas_call(
        pack_kernel,
        out_shape=(
            jax.ShapeDtypeStruct((occupied, LANES), jnp.bfloat16),
            jax.ShapeDtypeStruct(ov_rows.shape, jnp.bfloat16),
            jax.ShapeDtypeStruct(screened.shape, jnp.bfloat16),
        ),
        in_specs=[hbm()] * 3,
        out_specs=(vmem(),) * 3,
        scratch_shapes=[pltpu.VMEM(trials.shape, jnp.bfloat16), pltpu.SemaphoreType.DMA((3,))],
        compiler_params=pltpu.CompilerParams(vmem_limit_bytes=54960 << 10),
        name="pack",
    )(trials, ov_rows, screened)

    far = lax.ppermute(block, "half", cores)
    screened_peer = lax.ppermute(screened_held, "grp", cores)
    vv_peer = lax.ppermute(vv_factors, "grp", cores)

    far, screened_peer = lax.optimization_barrier((far, screened_peer))
    both = jnp.broadcast_to(jnp.stack([block, far])[None], (peers, 2, occupied, LANES))
    both = lax.all_to_all(both, PLANE, 0, 0, tiled=True, axis_index_groups=[plane])

    flops = 2 * 2 * functions * virt * virt_all * occupied
    terms = pl.pallas_call(
        lambda *refs: term_kernel(plane, window, *refs),
        out_shape=jax.ShapeDtypeStruct((groups, row_share, virt), jnp.bfloat16),
        in_specs=[vmem(), hbm(), hbm(), vmem(), vmem(), vmem()],
        out_specs=vmem(),
        scratch_shapes=[
            pltpu.VMEM((occupied, virt_all), jnp.bfloat16),
            pltpu.VMEM((2 * functions * ROWS, virt_all), jnp.bfloat16),
            pltpu.SemaphoreType.DMA((2 * functions,)),
        ],
        compiler_params=pltpu.CompilerParams(vmem_limit_bytes=52 << 20),
        cost_estimate=pl.CostEstimate(flops=flops, bytes_accessed=8 << 20, transcendentals=0),
        name="terms",
    )(both, vv_factors, vv_peer, screened_held, screened_peer, ov_held)

    terms, occ_energy, virt_energy, occ_order, virt_order = lax.optimization_barrier(
        (terms, occ_energy, virt_energy, occ_order, virt_order)
    )
    terms = lax.all_to_all(terms, WINDOW, 0, 0, tiled=True, axis_index_groups=[window])

    base = level_part(trials, occ_energy, virt_energy, occ_order, virt_order, row_offset, row_share)
    return pl.pallas_call(
        finish_kernel,
        out_shape=jax.ShapeDtypeStruct((row_share, virt), jnp.float32),
        in_specs=[vmem()] * 2,
        out_specs=vmem(),
        compiler_params=pltpu.CompilerParams(vmem_limit_bytes=8 << 20),
        name="finish",
    )(terms, base)


def solution(mesh):
    torus = Mesh(
        mesh.devices.reshape(2, 4, 4, mesh.shape["aux"], mesh.shape["grp"]),
        ("half", "x", "y", "aux", "grp"),
    )
    placed = (
        P(None, VROW),
        P(WINDOW, VROW, None),
        P(WINDOW, None, None),
        P(WINDOW, VROW, None),
        P(),
        P(),
        P(),
        P(VROW),
    )

    return jax.shard_map(on_device, mesh=torus, in_specs=placed, out_specs=P(WINDOW, VROW), check_vma=False)
```

profile of v0, /device:TPU:1, one launch (start us, length us, event | category | flops | bytes accessed | tf_op | source)
XLA Modules:
  0.0 69.0 jit_solution(6226269376120898744)
XLA Ops:
  0.0 0.0 copy-start
  0.0 8.9 %collective-permute-start.2 = (bf16[4,120,3840]{2,1,0:T(8,128)(2,1)}, bf16[4,120,3840]{2,1,0:T(8,128)(2,1)}, u32[]{:S(2)}, u32[]{:S(2)}) collective-permute-start(bf16[4,120,3840]{2,1,0:T(8,128)(2,1)} %refs_1_.1), channel_id=1, source_target_pairs={{0,1},{1,0},{2,3},{3,2},{4,5},{5,4},{6,7},{7,6},{8,9},{9,8},{10,11... | collective-permute-start | bytes 11059208 | tf_op jit(solution)/shard_map/ppermute | solution.py:203
  8.9 0.0 copy-start.1
  8.9 0.8 %copy-done.1 = bf16[192,120]{1,0:T(8,128)(2,1)S(1)} copy-done((bf16[192,120]{1,0:T(8,128)(2,1)S(1)}, bf16[192,120]{1,0:T(8,128)(2,1)}, u32[]{:S(2)}) %copy-start.1) | copy-done | bytes 46104
  9.7 1.2 %pack.1 = (bf16[96,128]{1,0:T(8,128)(2,1)S(1)}, bf16[4,96,120]{2,1,0:T(8,128)(2,1)S(1)}, bf16[4,96,96]{2,1,0:T(8,128)(2,1)S(1)}) custom-call(bf16[192,120]{1,0:T(8,128)(2,1)S(1)} %copy-done.1, bf16[4,96,120]{2,1,0:T(8,128)(2,1)} %bitcast.16, bf16[4,96,96]{2,1,0:T(8,128)(2,1)} %screened_hbm.1), custom_call_target="tpu_custom_call" | custom-call | tf_op jit(solution)/shard_map/pack/pallas_call | solution.py:187
  10.9 1.9 %collective-permute-start.1 = (bf16[4,96,96]{2,1,0:T(8,128)(2,1)S(1)}, bf16[4,96,96]{2,1,0:T(8,128)(2,1)S(1)}, u32[]{:S(2)}, u32[]{:S(2)}) collective-permute-start(bf16[4,96,96]{2,1,0:T(8,128)(2,1)S(1)} %get-tuple-element.16.refs_3_), channel_id=1, source_target_pairs={{0,1},{1,0},{2,3},{3,2},{4,5},{5,4},{6,7},{7,6},{8,9},{9,8},{10,11... | collective-permute-start | bytes 221192 | tf_op jit(solution)/shard_map/ppermute | solution.py:202
  12.9 10.1 %collective-permute-start = (bf16[96,128]{1,0:T(8,128)(2,1)S(1)}, bf16[96,128]{1,0:T(8,128)(2,1)S(1)}, u32[]{:S(2)}, u32[]{:S(2)}) collective-permute-start(bf16[96,128]{1,0:T(8,128)(2,1)S(1)} %get-tuple-element.15), channel_id=1, source_target_pairs={{0,256},{256,0},{1,257},{257,1},{2,258},{258,2},{3,259},{259,3},{4... | collective-permute-start | bytes 73736 | tf_op jit(solution)/shard_map/ppermute | solution.py:201
  23.0 3.2 %collective-permute-done = bf16[96,128]{1,0:T(8,128)(2,1)S(1)} collective-permute-done((bf16[96,128]{1,0:T(8,128)(2,1)S(1)}, bf16[96,128]{1,0:T(8,128)(2,1)S(1)}, u32[]{:S(2)}, u32[]{:S(2)}) %collective-permute-start) | collective-permute-done | bytes 24608 | tf_op jit(solution)/shard_map/ppermute | solution.py:201
  26.2 0.0 collective-permute-done.1.refs_4_
  26.2 1.0 %broadcast_in_dim.2 = bf16[16,2,96,128]{3,2,1,0:T(8,128)(2,1)} broadcast(bf16[2,96,128]{2,1,0:T(8,128)(2,1)S(1)} %pad_maximum_fusion), dimensions={1,2,3} | broadcast | bytes 835584 | tf_op jit(solution)/shard_map/broadcast_in_dim | solution.py:206
  27.2 6.9 %all-to-all-start = ((bf16[16,2,96,128]{3,2,1,0:T(8,128)(2,1)}), bf16[16,2,96,128]{3,2,1,0:T(8,128)(2,1)S(1)}, u32[]{:S(2)}, u32[]{:S(2)}) async-start(bf16[16,2,96,128]{3,2,1,0:T(8,128)(2,1)} %broadcast_in_dim.2), calls=%async_computation | async-start | bytes 1572864 | tf_op jit(solution)/shard_map/all_to_all | solution.py:207
  34.1 8.2 %all-to-all-done.refs_0_ = bf16[16,2,96,128]{3,2,1,0:T(8,128)(2,1)S(1)} async-done(((bf16[16,2,96,128]{3,2,1,0:T(8,128)(2,1)}), bf16[16,2,96,128]{3,2,1,0:T(8,128)(2,1)S(1)}, u32[]{:S(2)}, u32[]{:S(2)}) %all-to-all-start) | async-done | bytes 786464 | tf_op jit(solution)/shard_map/all_to_all | solution.py:207
  42.2 0.0 collective-permute-done.2.refs_2_
  42.3 0.0 copy-start.2
  42.3 0.0 copy-start.3
  42.3 0.0 copy-start.4
  42.3 7.2 %terms.1 = bf16[16,12,120]{2,1,0:T(8,128)(2,1)} custom-call(bf16[16,2,96,128]{3,2,1,0:T(8,128)(2,1)S(1)} %all-to-all-done.refs_0_, bf16[4,120,3840]{2,1,0:T(8,128)(2,1)} %refs_1_.1, bf16[4,120,3840]{2,1,0:T(8,128)(2,1)} %collective-permute-done.2.refs_2_, bf16[4,96,96]{2,1,0:T(8,128)(2,1)S(1)} %get-tuple-element.16.refs_3_, ...), custom_call_target="tpu_custom_call" | custom-call | flops 707788800 | bytes 8388608 | tf_op jit(solution)/shard_map/terms/pallas_call | solution.py:210
  49.5 0.0 copy-done.2
  49.5 11.5 %all-to-all-start.1 = ((bf16[16,12,120]{2,1,0:T(8,128)(2,1)}), bf16[16,12,120]{2,1,0:T(8,128)(2,1)S(1)}, u32[]{:S(2)}, u32[]{:S(2)}) async-start(bf16[16,12,120]{2,1,0:T(8,128)(2,1)} %terms.1), calls=%async_computation.1 | async-start | bytes 131072 | tf_op jit(solution)/shard_map/all_to_all | solution.py:228
  61.0 0.0 copy-done
  61.0 0.0 copy-done.3
  61.0 0.2 convolution_bitcast_fusion.1
  61.2 0.2 convolution_bitcast_fusion
  61.4 0.0 copy-done.4
  61.4 1.0 %fusion.1 = f32[120]{0:T(128)S(1)} fusion(f32[3840,1]{0,1:T(1,128)S(1)} %reshape.15, s32[120]{0:T(128)S(1)} %copy-done.4), kind=kOutput, calls=%fused_computation.4 | convolution fusion | flops 5990400 | bytes 16320 | tf_op jit(solution)/shard_map/dot_general | solution.py:161
  62.4 0.8 %convert_multiply_fusion.base_ref = f32[12,120]{1,0:T(8,128)S(1)} fusion(bf16[192,120]{1,0:T(8,128)(2,1)} %trials_hbm.1, s32[]{:T(128)S(6)} %select_n.15, f32[12]{0:T(128)S(1)} %convolution_bitcast_fusion, f32[120]{0:T(128)S(1)} %fusion.1), kind=kLoop, calls=%fused_computation.9 | loop fusion | flops 4320 | bytes 9172 | tf_op jit(solution)/shard_map/mul | solution.py:171
  63.2 5.1 %all-to-all-done.1.terms_ref = bf16[16,12,120]{2,1,0:T(8,128)(2,1)S(1)} async-done(((bf16[16,12,120]{2,1,0:T(8,128)(2,1)}), bf16[16,12,120]{2,1,0:T(8,128)(2,1)S(1)}, u32[]{:S(2)}, u32[]{:S(2)}) %all-to-all-start.1) | async-done | bytes 46112 | tf_op jit(solution)/shard_map/all_to_all | solution.py:228
  68.4 0.6 finish.1
  (3 shorter events, 0.0 us)
Async XLA Ops:
  0.0 61.0 %copy-start = (f32[96]{0:T(128)S(1)}, f32[96]{0:T(128)}, u32[]{:S(2)}) copy-start(f32[96]{0:T(128)} %param.12) | copy-start | bytes 1156
  0.0 42.2 %collective-permute-start.2 = (bf16[4,120,3840]{2,1,0:T(8,128)(2,1)}, bf16[4,120,3840]{2,1,0:T(8,128)(2,1)}, u32[]{:S(2)}, u32[]{:S(2)}) collective-permute-start(bf16[4,120,3840]{2,1,0:T(8,128)(2,1)} %refs_1_.1), channel_id=1, source_target_pairs={{0,1},{1,0},{2,3},{3,2},{4,5},{5,4},{6,7},{7,6},{8,9},{9,8},{10,11... | collective-permute-start | bytes 11059208 | tf_op jit(solution)/shard_map/ppermute | solution.py:203
  8.9 0.8 %copy-start.1 = (bf16[192,120]{1,0:T(8,128)(2,1)S(1)}, bf16[192,120]{1,0:T(8,128)(2,1)}, u32[]{:S(2)}) copy-start(bf16[192,120]{1,0:T(8,128)(2,1)} %trials_hbm.1) | copy-start | bytes 138244
  10.9 15.2 %collective-permute-start.1 = (bf16[4,96,96]{2,1,0:T(8,128)(2,1)S(1)}, bf16[4,96,96]{2,1,0:T(8,128)(2,1)S(1)}, u32[]{:S(2)}, u32[]{:S(2)}) collective-permute-start(bf16[4,96,96]{2,1,0:T(8,128)(2,1)S(1)} %get-tuple-element.16.refs_3_), channel_id=1, source_target_pairs={{0,1},{1,0},{2,3},{3,2},{4,5},{5,4},{6,7},{7,6},{8,9},{9,8},{10,11... | collective-permute-start | bytes 221192 | tf_op jit(solution)/shard_map/ppermute | solution.py:202
  12.9 13.3 %collective-permute-start = (bf16[96,128]{1,0:T(8,128)(2,1)S(1)}, bf16[96,128]{1,0:T(8,128)(2,1)S(1)}, u32[]{:S(2)}, u32[]{:S(2)}) collective-permute-start(bf16[96,128]{1,0:T(8,128)(2,1)S(1)} %get-tuple-element.15), channel_id=1, source_target_pairs={{0,256},{256,0},{1,257},{257,1},{2,258},{258,2},{3,259},{259,3},{4... | collective-permute-start | bytes 73736 | tf_op jit(solution)/shard_map/ppermute | solution.py:201
  27.2 15.1 %all-to-all-start = ((bf16[16,2,96,128]{3,2,1,0:T(8,128)(2,1)}), bf16[16,2,96,128]{3,2,1,0:T(8,128)(2,1)S(1)}, u32[]{:S(2)}, u32[]{:S(2)}) async-start(bf16[16,2,96,128]{3,2,1,0:T(8,128)(2,1)} %broadcast_in_dim.2), calls=%async_computation | async-start | bytes 1572864 | tf_op jit(solution)/shard_map/all_to_all | solution.py:207
  42.3 7.2 %copy-start.2 = (f32[3840]{0:T(1024)S(1)}, f32[3840]{0:T(1024)}, u32[]{:S(2)}) copy-start(f32[3840]{0:T(1024)} %param.13) | copy-start | bytes 46084
  42.3 18.7 %copy-start.3 = (s32[96]{0:T(128)S(1)}, s32[96]{0:T(128)}, u32[]{:S(2)}) copy-start(s32[96]{0:T(128)} %param.14) | copy-start | bytes 1156
  42.3 19.1 %copy-start.4 = (s32[120]{0:T(128)S(1)}, s32[120]{0:T(128)}, u32[]{:S(2)}) copy-start(s32[120]{0:T(128)} %param.15) | copy-start | bytes 1444
  49.5 18.9 %all-to-all-start.1 = ((bf16[16,12,120]{2,1,0:T(8,128)(2,1)}), bf16[16,12,120]{2,1,0:T(8,128)(2,1)S(1)}, u32[]{:S(2)}, u32[]{:S(2)}) async-start(bf16[16,12,120]{2,1,0:T(8,128)(2,1)} %terms.1), calls=%async_computation.1 | async-start | bytes 131072 | tf_op jit(solution)/shard_map/all_to_all | solution.py:228
where the time goes:
time: 69.4 us; the launch traced here: 69 us
  starting transfers between devices  39.2 us (56%)
  waiting for transfers between devices  16.5 us (24%)
  Pallas kernels  9.08 us (13%)
  local copies, waits for them, and re-layouts  1.85 us (3%)
  matrix products  1.39 us (2%)
  other arithmetic  0.85 us (1%)
    all_to_all x1, starting transfers between devices, on_device(): lax.all_to_all(terms, WINDOW, 0, 0, tiled=True, axis_index_groups=[window])  11.5 us
    ppermute x1, starting transfers between devices, on_device(): far = lax.ppermute(block, 'half', cores)  10.1 us
    ppermute x1, starting transfers between devices, on_device(): vv_peer = lax.ppermute(vv_factors, 'grp', cores)  8.87 us
    all_to_all x1, waiting for transfers between devices, on_device(): lax.all_to_all(both, PLANE, 0, 0, tiled=True, axis_index_groups=[plane])  8.19 us
    pallas_call x1, Pallas kernels, on_device(): pl.pallas_call(lambda *refs: term_kernel(plane, window, *refs), out_shape...  7.21 us
    all_to_all x1, starting transfers between devices, on_device(): lax.all_to_all(both, PLANE, 0, 0, tiled=True, axis_index_groups=[plane])  6.85 us
    all_to_all x1, waiting for transfers between devices, on_device(): lax.all_to_all(terms, WINDOW, 0, 0, tiled=True, axis_index_groups=[window])  5.15 us
    ppermute x1, waiting for transfers between devices, on_device(): far = lax.ppermute(block, 'half', cores)  3.18 us
  transfers between devices with their start and end apart: 5, of which 3 were waited for; matrix products, arithmetic and copies ran while one was open for 5% of the time, Pallas kernels for 2%

commit v1 on v0

--- a/solution.py
+++ b/solution.py
@@ -11,6 +11,7 @@
 WINDOW = ("aux", "grp")
 LANES = 128
 ROWS = 128
+SUBLANES = 8
 PIECES = 3
 
 
@@ -74,27 +75,61 @@
     copies[2].wait()
 
 
-def term_kernel(
-    plane, window, both_ref, vv_hbm, vv_peer_hbm, screened_ref, screened_peer_ref, ov_ref, out_ref, whole_ref, held_ref, sems
-):
+def hold_kernel(vv_hbm, screened_ref, joint_ref, sems):
+    functions, virt, _ = vv_hbm.shape
+    copies = [
+        pltpu.make_async_copy(vv_hbm.at[q], joint_ref.at[q, pl.ds(0, virt), :], sems.at[q]) for q in range(functions)
+    ]
+    for copy in copies:
+        copy.start()
+    occupied = screened_ref.shape[1]
+    for q in range(functions):
+        for k in range(occupied // SUBLANES):
+            strip = screened_ref[q, pl.ds(k * SUBLANES, SUBLANES), :]
+            joint_ref[q, pl.ds(virt, SUBLANES), pl.ds(k * LANES, occupied)] = strip
+
+    for copy in copies:
+        copy.wait()
+
+
+def energy_part(trials_ref, occ_ref, virt_ref, occ_at_ref, virt_at_ref, base_ref):
+    virt, occupied = base_ref.shape[1], occ_ref.shape[1]
+    share = base_ref.shape[0]
+    place = lax.axis_index("aux") * lax.axis_size("grp") + lax.axis_index("grp")
+    own = trials_ref[...].astype(jnp.float32)
+    rows = own[:share]
+    for w in range(1, own.shape[0] // share):
+        rows = jnp.where(place == w, own[w * share : (w + 1) * share], rows)
+
+    pad = jnp.zeros((1, LANES - virt), jnp.int32)
+    at = jnp.broadcast_to(jnp.concatenate([virt_at_ref[...], pad], axis=1), (SUBLANES, LANES))
+    group, lane_at = at // LANES, at % LANES
+    sublane = lax.broadcasted_iota(jnp.int32, (SUBLANES, LANES), 0)
+    levels = jnp.zeros((SUBLANES, LANES), jnp.float32)
+    count = virt_ref.shape[0]
+    for k in range(0, count, SUBLANES):
+        size = min(SUBLANES, count - k)
+        table = virt_ref[pl.ds(k, size), :]
+        if size < SUBLANES:
+            table = jnp.concatenate([table, jnp.zeros((SUBLANES - size, LANES), jnp.float32)], axis=0)
+        found = jnp.take_along_axis(table, lane_at, axis=1)
+        levels = levels + jnp.where(sublane + k == group, found, 0.0)
+    levels = jnp.sum(levels, axis=0, keepdims=True)[:, :virt]
+
+    lane = lax.broadcasted_iota(jnp.int32, (share, occupied), 1)
+    wanted = lax.rem(place * share, occupied) + lax.broadcasted_iota(jnp.int32, (share, occupied), 0)
+    entry = jnp.sum(jnp.where(lane == wanted, occ_at_ref[...].astype(jnp.float32), 0.0), axis=1, keepdims=True)
+    picked = lane.astype(jnp.float32) == entry
+    lower = jnp.sum(jnp.where(picked, occ_ref[...], 0.0), axis=1, keepdims=True)
+    base_ref[...] = (levels - lower) * rows
+
+
+def term_kernel(plane, window, both_ref, joint_ref, peer_ref, ov_ref, *refs):
+    *level_refs, out_ref, base_ref, whole_ref = refs
+    energy_part(*level_refs, base_ref)
     core = lax.axis_index("grp")
     half = lax.axis_index("half")
     functions, occupied, virt = ov_ref.shape
-    copies = [
-        [
-            pltpu.make_async_copy(
-                source.at[q],
-                held_ref.at[pl.ds((side * functions + q) * ROWS, virt), :],
-                sems.at[side * functions + q],
-            )
-            for q in range(functions)
-        ]
-        for side, source in enumerate((vv_hbm, vv_peer_hbm))
-    ]
-    for side in copies:
-        for copy in side:
-            copy.start()
-
     blocks = both_ref.shape[0]
     spare = LANES - virt
     tiles = blocks * virt // LANES
@@ -126,16 +161,17 @@
         other = other + factors * jnp.where(core == 0, second, first)
 
     turned = jnp.zeros((virt, occupied), jnp.float32)
-    for side, screen in enumerate((screened_ref, screened_peer_ref)):
-        for copy in copies[side]:
-            copy.wait()
-        factor = held_ref[pl.ds(side * functions * ROWS, functions * ROWS), :]
+    for ref in (joint_ref, peer_ref):
+        factor = ref[...].reshape(functions * ROWS, whole_ref.shape[1])
         image = lax.dot_general(factor, whole_ref[...], (((1,), (1,)), ((), ())), preferred_element_type=jnp.float32)
         image = image.astype(jnp.bfloat16)
         for q in range(functions):
-            turned = turned + jnp.dot(
-                image[q * ROWS : q * ROWS + virt], screen[q], preferred_element_type=jnp.float32
-            )
+            strips = [
+                ref[q, pl.ds(virt, SUBLANES), pl.ds(k * LANES, occupied)].astype(jnp.float32)
+                for k in range(occupied // SUBLANES)
+            ]
+            screen = jnp.concatenate(strips, axis=0).astype(jnp.bfloat16)
+            turned = turned + jnp.dot(image[q * ROWS : q * ROWS + virt], screen, preferred_element_type=jnp.float32)
     mine = mine - turned.T
 
     share = out_ref.shape[1]
@@ -155,35 +191,18 @@
     out_ref[...] = total
 
 
-def table_lookup(order, table):
-    columns = lax.broadcasted_iota(jnp.int32, (order.shape[0], table.shape[0]), 1)
-    picker = (order[:, None] == columns).astype(jnp.float32)
-    return jnp.dot(picker, table, precision=lax.Precision.HIGHEST)
-
-
-def level_part(trials, occ_energy, virt_energy, occ_order, virt_order, row_offset, row_share):
-    occupied = occ_energy.shape[0]
-    virt_levels = table_lookup(virt_order, virt_energy)
-    occ_levels = table_lookup(occ_order, occ_energy)
-    row_ids = row_offset + lax.broadcasted_iota(jnp.int32, (row_share,), 0)
-    row_levels = table_lookup(row_ids % occupied, occ_levels)
-    own_trials = lax.dynamic_slice_in_dim(trials, row_offset, row_share, 0).astype(jnp.float32)
-    return (virt_levels[None, :] - row_levels[:, None]) * own_trials
-
-
 def on_device(trials, vv_factors, screened, ov_factors, occ_energy, virt_energy, occ_order, virt_order):
     groups = lax.axis_size(WINDOW)
     rows_all, virt = trials.shape
     occupied = occ_energy.shape[0]
     functions, _, virt_all = vv_factors.shape
     row_share = rows_all // groups
-    row_offset = lax.axis_index(WINDOW) * row_share
-    ov_rows = jnp.swapaxes(ov_factors, 1, 2)
     peers = lax.axis_size(PLANE)
     window = window_order(groups)
     plane = plane_order(peers)
     cores = [(0, 1), (1, 0)]
 
+    ov_rows = jnp.swapaxes(ov_factors, 1, 2)
     block, ov_held, screened_held = pl.pallas_call(
         pack_kernel,
         out_shape=(
@@ -195,39 +214,54 @@
         out_specs=(vmem(),) * 3,
         scratch_shapes=[pltpu.VMEM(trials.shape, jnp.bfloat16), pltpu.SemaphoreType.DMA((3,))],
         compiler_params=pltpu.CompilerParams(vmem_limit_bytes=54960 << 10),
+        cost_estimate=pl.CostEstimate(flops=2 * 10**10, bytes_accessed=10**6, transcendentals=0),
         name="pack",
     )(trials, ov_rows, screened)
 
     far = lax.ppermute(block, "half", cores)
-    screened_peer = lax.ppermute(screened_held, "grp", cores)
-    vv_peer = lax.ppermute(vv_factors, "grp", cores)
-
-    far, screened_peer = lax.optimization_barrier((far, screened_peer))
+
+    joint = pl.pallas_call(
+        hold_kernel,
+        out_shape=jax.ShapeDtypeStruct((functions, ROWS, virt_all), jnp.bfloat16),
+        in_specs=[hbm(), vmem()],
+        out_specs=vmem(),
+        scratch_shapes=[pltpu.SemaphoreType.DMA((functions,))],
+        compiler_params=pltpu.CompilerParams(vmem_limit_bytes=8192 << 10),
+        cost_estimate=pl.CostEstimate(flops=10**8, bytes_accessed=8 << 20, transcendentals=0),
+        name="hold",
+    )(vv_factors, screened_held)
+    joint_peer = lax.ppermute(joint, "grp", cores)
+
     both = jnp.broadcast_to(jnp.stack([block, far])[None], (peers, 2, occupied, LANES))
     both = lax.all_to_all(both, PLANE, 0, 0, tiled=True, axis_index_groups=[plane])
 
     flops = 2 * 2 * functions * virt * virt_all * occupied
-    terms = pl.pallas_call(
+    terms, base = pl.pallas_call(
         lambda *refs: term_kernel(plane, window, *refs),
-        out_shape=jax.ShapeDtypeStruct((groups, row_share, virt), jnp.bfloat16),
-        in_specs=[vmem(), hbm(), hbm(), vmem(), vmem(), vmem()],
-        out_specs=vmem(),
-        scratch_shapes=[
-            pltpu.VMEM((occupied, virt_all), jnp.bfloat16),
-            pltpu.VMEM((2 * functions * ROWS, virt_all), jnp.bfloat16),
-            pltpu.SemaphoreType.DMA((2 * functions,)),
-        ],
-        compiler_params=pltpu.CompilerParams(vmem_limit_bytes=52 << 20),
+        out_shape=(
+            jax.ShapeDtypeStruct((groups, row_share, virt), jnp.bfloat16),
+            jax.ShapeDtypeStruct((row_share, virt), jnp.float32),
+        ),
+        in_specs=[vmem()] * 9,
+        out_specs=(vmem(),) * 2,
+        scratch_shapes=[pltpu.VMEM((occupied, virt_all), jnp.bfloat16)],
+        compiler_params=pltpu.CompilerParams(vmem_limit_bytes=8192 << 10),
         cost_estimate=pl.CostEstimate(flops=flops, bytes_accessed=8 << 20, transcendentals=0),
         name="terms",
-    )(both, vv_factors, vv_peer, screened_held, screened_peer, ov_held)
-
-    terms, occ_energy, virt_energy, occ_order, virt_order = lax.optimization_barrier(
-        (terms, occ_energy, virt_energy, occ_order, virt_order)
+    )(
+        both,
+        joint,
+        joint_peer,
+        ov_held,
+        trials,
+        occ_energy.reshape(1, -1),
+        virt_energy.reshape(-1, LANES),
+        occ_order.reshape(1, -1),
+        virt_order.reshape(1, -1),
     )
+
     terms = lax.all_to_all(terms, WINDOW, 0, 0, tiled=True, axis_index_groups=[window])
 
-    base = level_part(trials, occ_energy, virt_energy, occ_order, virt_order, row_offset, row_share)
     return pl.pallas_call(
         finish_kernel,
         out_shape=jax.ShapeDtypeStruct((row_share, virt), jnp.float32),

time: 69.4 us -> 64.5 us (0.929)
  blocking collectives: 0 us -> 32.9 us
  starting transfers between devices: 39.2 us -> 18.8 us
  waiting for transfers between devices: 16.5 us -> 3.18 us
  Pallas kernels: 9.08 us -> 7.47 us
  matrix products: 1.39 us -> 0 us
  other arithmetic: 0.85 us -> 0.01 us
    all_to_all x0 -> x2, blocking collectives: none -> 32.9 us  [the longest x1 18.1 us: on_device(): lax.all_to_all(terms, WINDOW, 0, 0, tiled=True, axis_index_groups=[window])]
    all_to_all x2 -> x0, starting transfers between devices: 18.3 us -> none  [the longest x1 11.5 us: on_device(): lax.all_to_all(terms, WINDOW, 0, 0, tiled=True, axis_index_groups=[window])]
    all_to_all x2 -> x0, waiting for transfers between devices: 13.3 us -> none  [the longest x1 8.19 us: on_device(): lax.all_to_all(both, PLANE, 0, 0, tiled=True, axis_index_groups=[plane])]
    pallas_call x1, Pallas kernels: 7.21 us -> 4.47 us  [on_device(): pl.pallas_call(lambda *refs: term_kernel(plane, window, *refs), out_shape...]
    ppermute x2 -> x1, starting transfers between devices: 10.8 us -> 8.75 us  [on_device(): joint_peer = lax.ppermute(joint, 'grp', cores)]
    dot_general x3 -> x0, matrix products: 1.39 us -> none  [table_lookup(): return jnp.dot(picker, table, precision=lax.Precision.HIGHEST)]
    pallas_call x0 -> x1, Pallas kernels: none -> 0.97 us  [on_device(): pl.pallas_call(hold_kernel, out_shape=jax.ShapeDtypeStruct((functions, RO...]
    broadcast_in_dim x1, local copies, waits for them, and re-layouts: 1.02 us -> 0.15 us  [on_device(): jnp.broadcast_to(jnp.stack([block, far])[None], (peers, 2, occupied, LANES))]
  transfers between devices with their start and end apart: 5 -> 2, of which waited for: 3 -> 1; matrix products, arithmetic and copies ran while one was open for 5% -> 0% of each run, Pallas kernels for 2% -> 0%
where the time goes in v1:
time: 64.5 us; the launch traced here: 64.2 us
  blocking collectives  32.9 us (51%)
  starting transfers between devices  18.8 us (29%)
  Pallas kernels  7.47 us (12%)
  waiting for transfers between devices  3.18 us (5%)
  local copies, waits for them, and re-layouts  1.68 us (3%)
    all_to_all x1, blocking collectives, on_device(): lax.all_to_all(terms, WINDOW, 0, 0, tiled=True, axis_index_groups=[window])  18.1 us
    all_to_all x1, blocking collectives, on_device(): lax.all_to_all(both, PLANE, 0, 0, tiled=True, axis_index_groups=[plane])  14.8 us
    ppermute x1, starting transfers between devices, on_device(): far = lax.ppermute(block, 'half', cores)  10.1 us
    ppermute x1, starting transfers between devices, on_device(): joint_peer = lax.ppermute(joint, 'grp', cores)  8.75 us
    pallas_call x1, Pallas kernels, on_device(): pl.pallas_call(lambda *refs: term_kernel(plane, window, *refs), out_shape...  4.47 us
    ppermute x1, waiting for transfers between devices, on_device(): far = lax.ppermute(block, 'half', cores)  3.18 us
    unnamed x12, local copies, waits for them, and re-layouts  1.53 us
    pallas_call x1, Pallas kernels, on_device(): pl.pallas_call(pack_kernel, out_shape=(jax.ShapeDtypeStruct((occupied, LA...  1.41 us
  transfers between devices with their start and end apart: 2, of which 1 were waited for; matrix products, arithmetic and copies ran while one was open for 0% of the time, Pallas kernels for 0%

profile of v1, /device:TPU:1, one launch (start us, length us, event | category | flops | bytes accessed | tf_op | source)
XLA Modules:
  0.0 64.2 jit_solution(14446921416834205304)
XLA Ops:
  0.0 0.0 copy-start.1
  0.0 0.8 %copy-done.1 = bf16[192,120]{1,0:T(8,128)(2,1)S(1)} copy-done((bf16[192,120]{1,0:T(8,128)(2,1)S(1)}, bf16[192,120]{1,0:T(8,128)(2,1)}, u32[]{:S(2)}) %copy-start.1) | copy-done | bytes 46104
  0.8 0.0 copy-start
  0.8 1.4 %pack.1 = (bf16[96,128]{1,0:T(8,128)(2,1)S(1)}, bf16[4,96,120]{2,1,0:T(8,128)(2,1)S(1)}, bf16[4,96,96]{2,1,0:T(8,128)(2,1)S(1)}) custom-call(bf16[192,120]{1,0:T(8,128)(2,1)S(1)} %copy-done.1, bf16[4,96,120]{2,1,0:T(8,128)(2,1)} %bitcast.13, bf16[4,96,96]{2,1,0:T(8,128)(2,1)} %screened_hbm.1), custom_call_target="tpu_custom_call" | custom-call | flops 20000000000 | bytes 1000000 | tf_op jit(solution)/shard_map/pack/pallas_call | solution.py:206
  2.2 0.7 %copy-done = bf16[4,120,3840]{2,1,0:T(8,128)(2,1)S(1)} copy-done((bf16[4,120,3840]{2,1,0:T(8,128)(2,1)S(1)}, bf16[4,120,3840]{2,1,0:T(8,128)(2,1)}, u32[]{:S(2)}) %copy-start) | copy-done | bytes 3686424
  2.9 0.0 copy-start.2
  2.9 0.0 copy-start.3
  2.9 0.0 copy-start.4
  2.9 0.0 copy-start.5
  2.9 1.0 %hold.1.refs_1_ = bf16[4,128,3840]{2,1,0:T(8,128)(2,1)S(1)} custom-call(bf16[4,120,3840]{2,1,0:T(8,128)(2,1)S(1)} %copy-done, bf16[4,96,96]{2,1,0:T(8,128)(2,1)S(1)} %get-tuple-element.11.screened_ref), custom_call_target="tpu_custom_call" | custom-call | flops 100000000 | bytes 8388608 | tf_op jit(solution)/shard_map/hold/pallas_call | solution.py:223
  3.9 8.7 %collective-permute-start.1 = (bf16[4,128,3840]{2,1,0:T(8,128)(2,1)S(1)}, bf16[4,128,3840]{2,1,0:T(8,128)(2,1)S(1)}, u32[]{:S(2)}, u32[]{:S(2)}) collective-permute-start(bf16[4,128,3840]{2,1,0:T(8,128)(2,1)S(1)} %hold.1.refs_1_), channel_id=1, source_target_pairs={{0,1},{1,0},{2,3},{3,2},{4,5},{5,4},{6,7},{7,6},{8,9},{9,8},{10,11... | collective-permute-start | bytes 11796488 | tf_op jit(solution)/shard_map/ppermute | solution.py:233
  12.7 10.1 %collective-permute-start = (bf16[96,128]{1,0:T(8,128)(2,1)S(1)}, bf16[96,128]{1,0:T(8,128)(2,1)S(1)}, u32[]{:S(2)}, u32[]{:S(2)}) collective-permute-start(bf16[96,128]{1,0:T(8,128)(2,1)S(1)} %get-tuple-element.10), channel_id=1, source_target_pairs={{0,256},{256,0},{1,257},{257,1},{2,258},{258,2},{3,259},{259,3},{4... | collective-permute-start | bytes 73736 | tf_op jit(solution)/shard_map/ppermute | solution.py:221
  22.8 3.2 %collective-permute-done = bf16[96,128]{1,0:T(8,128)(2,1)S(1)} collective-permute-done((bf16[96,128]{1,0:T(8,128)(2,1)S(1)}, bf16[96,128]{1,0:T(8,128)(2,1)S(1)}, u32[]{:S(2)}, u32[]{:S(2)}) %collective-permute-start) | collective-permute-done | bytes 24608 | tf_op jit(solution)/shard_map/ppermute | solution.py:221
  26.0 0.1 broadcast_in_dim.2
  26.1 14.8 %all_to_all.10.refs_0_ = bf16[16,2,96,128]{3,2,1,0:T(8,128)(2,1)S(1)} all-to-all(bf16[16,2,96,128]{3,2,1,0:T(8,128)(2,1)S(1)} %broadcast_in_dim.2), channel_id=1, replica_groups={{160,0,16,32,48,64,80,96,112,128,144,176,192,208,224,240},{161,1,17,33,..., dimensions={0} | all-to-all | bytes 1572864 | tf_op jit(solution)/shard_map/all_to_all | solution.py:236
  40.9 0.0 collective-permute-done.1.refs_2_
  40.9 0.0 copy-done.2
  40.9 0.0 copy-done.3
  40.9 0.0 copy-done.4
  40.9 0.0 copy-done.5
  40.9 4.5 %terms.1 = (bf16[16,12,120]{2,1,0:T(8,128)(2,1)S(1)}, f32[12,120]{1,0:T(8,128)S(1)}) custom-call(bf16[16,2,96,128]{3,2,1,0:T(8,128)(2,1)S(1)} %all_to_all.10.refs_0_, bf16[4,128,3840]{2,1,0:T(8,128)(2,1)S(1)} %hold.1.refs_1_, bf16[4,128,3840]{2,1,0:T(8,128)(2,1)S(1)} %collective-permute-done.1.refs_2_, bf16[4,96,120]{2,1,0:T(8,128)(2,1)S(1)} %get-tuple-element.12.refs_3_, ...), custom_call_target="tpu_custom_call" | custom-call | flops 707788800 | bytes 8388608 | tf_op jit(solution)/shard_map/terms/pallas_call | solution.py:239
  45.4 18.1 %all_to_all.11.terms_ref = bf16[16,12,120]{2,1,0:T(8,128)(2,1)S(1)} all-to-all(bf16[16,12,120]{2,1,0:T(8,128)(2,1)S(1)} %get-tuple-element.13), channel_id=1, replica_groups={{7,9,6,8,5,11,4,10,3,13,2,12,1,15,0,14},{23,25,22,24,21,27,20,26,19,29,..., dimensions={0} | all-to-all | bytes 92160 | tf_op jit(solution)/shard_map/all_to_all | solution.py:263
  63.6 0.6 finish.1
  (1 shorter events, 0.0 us)
Async XLA Ops:
  0.0 0.8 %copy-start.1 = (bf16[192,120]{1,0:T(8,128)(2,1)S(1)}, bf16[192,120]{1,0:T(8,128)(2,1)}, u32[]{:S(2)}) copy-start(bf16[192,120]{1,0:T(8,128)(2,1)} %refs_4_.1) | copy-start | bytes 138244
  0.8 2.1 %copy-start = (bf16[4,120,3840]{2,1,0:T(8,128)(2,1)S(1)}, bf16[4,120,3840]{2,1,0:T(8,128)(2,1)}, u32[]{:S(2)}) copy-start(bf16[4,120,3840]{2,1,0:T(8,128)(2,1)} %vv_hbm.1) | copy-start | bytes 11059204
  2.9 38.0 %copy-start.2 = (f32[3840]{0:T(1024)S(1)}, f32[3840]{0:T(1024)}, u32[]{:S(2)}) copy-start(f32[3840]{0:T(1024)} %param.13) | copy-start | bytes 46084
  2.9 38.0 %copy-start.3 = (f32[96]{0:T(128)S(1)}, f32[96]{0:T(128)}, u32[]{:S(2)}) copy-start(f32[96]{0:T(128)} %param.12) | copy-start | bytes 1156
  2.9 38.0 %copy-start.4 = (s32[96]{0:T(128)S(1)}, s32[96]{0:T(128)}, u32[]{:S(2)}) copy-start(s32[96]{0:T(128)} %param.14) | copy-start | bytes 1156
  2.9 38.0 %copy-start.5 = (s32[120]{0:T(128)S(1)}, s32[120]{0:T(128)}, u32[]{:S(2)}) copy-start(s32[120]{0:T(128)} %param.15) | copy-start | bytes 1444
  3.9 37.0 %collective-permute-start.1 = (bf16[4,128,3840]{2,1,0:T(8,128)(2,1)S(1)}, bf16[4,128,3840]{2,1,0:T(8,128)(2,1)S(1)}, u32[]{:S(2)}, u32[]{:S(2)}) collective-permute-start(bf16[4,128,3840]{2,1,0:T(8,128)(2,1)S(1)} %hold.1.refs_1_), channel_id=1, source_target_pairs={{0,1},{1,0},{2,3},{3,2},{4,5},{5,4},{6,7},{7,6},{8,9},{9,8},{10,11... | collective-permute-start | bytes 11796488 | tf_op jit(solution)/shard_map/ppermute | solution.py:233
  12.7 13.3 %collective-permute-start = (bf16[96,128]{1,0:T(8,128)(2,1)S(1)}, bf16[96,128]{1,0:T(8,128)(2,1)S(1)}, u32[]{:S(2)}, u32[]{:S(2)}) collective-permute-start(bf16[96,128]{1,0:T(8,128)(2,1)S(1)} %get-tuple-element.10), channel_id=1, source_target_pairs={{0,256},{256,0},{1,257},{257,1},{2,258},{258,2},{3,259},{259,3},{4... | collective-permute-start | bytes 73736 | tf_op jit(solution)/shard_map/ppermute | solution.py:221

commit v2 on v1

--- a/solution.py
+++ b/solution.py
@@ -47,15 +47,14 @@
     return [first, *(place for place in range(count) if place != first)]
 
 
-def pack_kernel(trials_hbm, ov_hbm, screened_hbm, block_ref, ov_ref, screened_ref, trials_ref, sems):
+def pack_kernel(trials_hbm, ov_hbm, block_ref, trials_ref, ov_ref, sems):
     copies = [
         pltpu.make_async_copy(trials_hbm, trials_ref, sems.at[0]),
         pltpu.make_async_copy(ov_hbm, ov_ref, sems.at[1]),
-        pltpu.make_async_copy(screened_hbm, screened_ref, sems.at[2]),
     ]
     for copy in copies:
         copy.start()
-    for copy in copies[:2]:
+    for copy in copies:
         copy.wait()
     core = lax.axis_index("grp")
     row = (lax.axis_index("half") * lax.axis_size("x") + lax.axis_index("x")) * lax.axis_size("y") + lax.axis_index("y")
@@ -72,7 +71,6 @@
     wide = jnp.concatenate([own, jnp.broadcast_to(column, (occupied, spare))], axis=1)
     turn = lax.rem(row * virt, LANES)
     block_ref[...] = pltpu.roll(wide, turn, 1).astype(jnp.bfloat16)
-    copies[2].wait()
 
 
 def hold_kernel(vv_hbm, screened_ref, joint_ref, sems):
@@ -126,7 +124,6 @@
 
 def term_kernel(plane, window, both_ref, joint_ref, peer_ref, ov_ref, *refs):
     *level_refs, out_ref, base_ref, whole_ref = refs
-    energy_part(*level_refs, base_ref)
     core = lax.axis_index("grp")
     half = lax.axis_index("half")
     functions, occupied, virt = ov_ref.shape
@@ -152,6 +149,25 @@
     pair = jnp.sum(gathered, axis=1, keepdims=True) * (2.0 / spare)
     pair = sum(pair[k * entries : (k + 1) * entries] for k in range(PIECES))
 
+    def contracted(ref):
+        factor = ref[...].reshape(functions * ROWS, whole_ref.shape[1])
+        image = lax.dot_general(factor, whole_ref[...], (((1,), (1,)), ((), ())), preferred_element_type=jnp.float32)
+        return image.astype(jnp.bfloat16)
+
+    def screened(image, ref):
+        total = jnp.zeros((virt, occupied), jnp.float32)
+        for q in range(functions):
+            strips = [
+                ref[q, pl.ds(virt, SUBLANES), pl.ds(k * LANES, occupied)].astype(jnp.float32)
+                for k in range(occupied // SUBLANES)
+            ]
+            screen = jnp.concatenate(strips, axis=0).astype(jnp.bfloat16)
+            total = total + jnp.dot(image[q * ROWS : q * ROWS + virt], screen, preferred_element_type=jnp.float32)
+        return total
+
+    own = contracted(joint_ref)
+    peer = contracted(peer_ref)
+    turned = screened(own, joint_ref)
     mine = jnp.zeros((occupied, virt), jnp.float32)
     other = jnp.zeros((occupied, virt), jnp.float32)
     for q in range(functions):
@@ -160,18 +176,8 @@
         mine = mine + factors * jnp.where(core == 0, first, second)
         other = other + factors * jnp.where(core == 0, second, first)
 
-    turned = jnp.zeros((virt, occupied), jnp.float32)
-    for ref in (joint_ref, peer_ref):
-        factor = ref[...].reshape(functions * ROWS, whole_ref.shape[1])
-        image = lax.dot_general(factor, whole_ref[...], (((1,), (1,)), ((), ())), preferred_element_type=jnp.float32)
-        image = image.astype(jnp.bfloat16)
-        for q in range(functions):
-            strips = [
-                ref[q, pl.ds(virt, SUBLANES), pl.ds(k * LANES, occupied)].astype(jnp.float32)
-                for k in range(occupied // SUBLANES)
-            ]
-            screen = jnp.concatenate(strips, axis=0).astype(jnp.bfloat16)
-            turned = turned + jnp.dot(image[q * ROWS : q * ROWS + virt], screen, preferred_element_type=jnp.float32)
+    energy_part(*level_refs, base_ref)
+    turned = turned + screened(peer, peer_ref)
     mine = mine - turned.T
 
     share = out_ref.shape[1]
@@ -203,20 +209,20 @@
     cores = [(0, 1), (1, 0)]
 
     ov_rows = jnp.swapaxes(ov_factors, 1, 2)
-    block, ov_held, screened_held = pl.pallas_call(
+    block = pl.pallas_call(
         pack_kernel,
-        out_shape=(
-            jax.ShapeDtypeStruct((occupied, LANES), jnp.bfloat16),
-            jax.ShapeDtypeStruct(ov_rows.shape, jnp.bfloat16),
-            jax.ShapeDtypeStruct(screened.shape, jnp.bfloat16),
-        ),
-        in_specs=[hbm()] * 3,
-        out_specs=(vmem(),) * 3,
-        scratch_shapes=[pltpu.VMEM(trials.shape, jnp.bfloat16), pltpu.SemaphoreType.DMA((3,))],
-        compiler_params=pltpu.CompilerParams(vmem_limit_bytes=54960 << 10),
+        out_shape=jax.ShapeDtypeStruct((occupied, LANES), jnp.bfloat16),
+        in_specs=[hbm()] * 2,
+        out_specs=vmem(),
+        scratch_shapes=[
+            pltpu.VMEM(trials.shape, jnp.bfloat16),
+            pltpu.VMEM(ov_rows.shape, jnp.bfloat16),
+            pltpu.SemaphoreType.DMA((2,)),
+        ],
+        compiler_params=pltpu.CompilerParams(vmem_limit_bytes=55200 << 10),
         cost_estimate=pl.CostEstimate(flops=2 * 10**10, bytes_accessed=10**6, transcendentals=0),
         name="pack",
-    )(trials, ov_rows, screened)
+    )(trials, ov_rows)
 
     far = lax.ppermute(block, "half", cores)
 
@@ -229,7 +235,7 @@
         compiler_params=pltpu.CompilerParams(vmem_limit_bytes=8192 << 10),
         cost_estimate=pl.CostEstimate(flops=10**8, bytes_accessed=8 << 20, transcendentals=0),
         name="hold",
-    )(vv_factors, screened_held)
+    )(vv_factors, screened)
     joint_peer = lax.ppermute(joint, "grp", cores)
 
     both = jnp.broadcast_to(jnp.stack([block, far])[None], (peers, 2, occupied, LANES))
@@ -252,7 +258,7 @@
         both,
         joint,
         joint_peer,
-        ov_held,
+        ov_rows,
         trials,
         occ_energy.reshape(1, -1),
         virt_energy.reshape(-1, LANES),

time: 64.5 us -> 63.9 us (level)
  Pallas kernels: 7.47 us -> 5.38 us
  local copies, waits for them, and re-layouts: 1.68 us -> 3.12 us
    pallas_call x1, Pallas kernels: 4.47 us -> 2.5 us  [on_device(): pl.pallas_call(lambda *refs: term_kernel(plane, window, *refs), out_shape...]
    unnamed x12 -> x16, local copies, waits for them, and re-layouts: 1.53 us -> 2.97 us
  transfers between devices with their start and end apart: 2 -> 2, of which waited for: 1 -> 1; matrix products, arithmetic and copies ran while one was open for 0% -> 0% of each run, Pallas kernels for 0% -> 2%
where the time goes in v2:
time: 63.9 us; the launch traced here: 63.6 us
  blocking collectives  32.9 us (51%)
  starting transfers between devices  18.8 us (29%)
  Pallas kernels  5.38 us (8%)
  waiting for transfers between devices  3.18 us (5%)
  local copies, waits for them, and re-layouts  3.12 us (5%)
    all_to_all x1, blocking collectives, on_device(): lax.all_to_all(terms, WINDOW, 0, 0, tiled=True, axis_index_groups=[window])  18.1 us
    all_to_all x1, blocking collectives, on_device(): lax.all_to_all(both, PLANE, 0, 0, tiled=True, axis_index_groups=[plane])  14.8 us
    ppermute x1, starting transfers between devices, on_device(): far = lax.ppermute(block, 'half', cores)  10.1 us
    ppermute x1, starting transfers between devices, on_device(): joint_peer = lax.ppermute(joint, 'grp', cores)  8.75 us
    ppermute x1, waiting for transfers between devices, on_device(): far = lax.ppermute(block, 'half', cores)  3.18 us
    unnamed x16, local copies, waits for them, and re-layouts  2.97 us
    pallas_call x1, Pallas kernels, on_device(): pl.pallas_call(lambda *refs: term_kernel(plane, window, *refs), out_shape...  2.5 us
    pallas_call x1, Pallas kernels, on_device(): pl.pallas_call(pack_kernel, out_shape=jax.ShapeDtypeStruct((occupied, LAN...  1.29 us
  transfers between devices with their start and end apart: 2, of which 1 were waited for; matrix products, arithmetic and copies ran while one was open for 0% of the time, Pallas kernels for 2%

profile of v2, /device:TPU:1, one launch (start us, length us, event | category | flops | bytes accessed | tf_op | source)
XLA Modules:
  0.0 63.6 jit_solution(8548274912647238167)
XLA Ops:
  0.0 0.0 copy-start
  0.0 2.0 %copy-done = bf16[4,120,3840]{2,1,0:T(8,128)(2,1)S(1)} copy-done((bf16[4,120,3840]{2,1,0:T(8,128)(2,1)S(1)}, bf16[4,120,3840]{2,1,0:T(8,128)(2,1)}, u32[]{:S(2)}) %copy-start) | copy-done | bytes 3686424
  2.0 0.0 copy-start.1
  2.0 0.9 %copy-done.1 = bf16[4,96,96]{2,1,0:T(8,128)(2,1)S(1)} copy-done((bf16[4,96,96]{2,1,0:T(8,128)(2,1)S(1)}, bf16[4,96,96]{2,1,0:T(8,128)(2,1)}, u32[]{:S(2)}) %copy-start.1) | copy-done | bytes 73752
  2.9 1.0 %hold.1.refs_1_ = bf16[4,128,3840]{2,1,0:T(8,128)(2,1)S(1)} custom-call(bf16[4,120,3840]{2,1,0:T(8,128)(2,1)S(1)} %copy-done, bf16[4,96,96]{2,1,0:T(8,128)(2,1)S(1)} %copy-done.1), custom_call_target="tpu_custom_call" | custom-call | flops 100000000 | bytes 8388608 | tf_op jit(solution)/shard_map/hold/pallas_call | solution.py:229
  3.9 8.7 %collective-permute-start.1 = (bf16[4,128,3840]{2,1,0:T(8,128)(2,1)S(1)}, bf16[4,128,3840]{2,1,0:T(8,128)(2,1)S(1)}, u32[]{:S(2)}, u32[]{:S(2)}) collective-permute-start(bf16[4,128,3840]{2,1,0:T(8,128)(2,1)S(1)} %hold.1.refs_1_), channel_id=1, source_target_pairs={{0,1},{1,0},{2,3},{3,2},{4,5},{5,4},{6,7},{7,6},{8,9},{9,8},{10,11... | collective-permute-start | bytes 11796488 | tf_op jit(solution)/shard_map/ppermute | solution.py:239
  12.7 0.0 copy-start.2
  12.7 0.0 copy-start.3
  12.7 0.0 copy-start.4
  12.7 0.0 copy-start.5
  12.7 0.0 copy-start.6
  12.7 0.0 copy-start.7
  12.7 1.3 %pack.1 = bf16[96,128]{1,0:T(8,128)(2,1)S(1)} custom-call(bf16[192,120]{1,0:T(8,128)(2,1)} %refs_4_.1, bf16[4,96,120]{2,1,0:T(8,128)(2,1)} %bitcast.7), custom_call_target="tpu_custom_call" | custom-call | flops 20000000000 | bytes 1000000 | tf_op jit(solution)/shard_map/pack/pallas_call | solution.py:212
  14.0 10.1 %collective-permute-start = (bf16[96,128]{1,0:T(8,128)(2,1)S(1)}, bf16[96,128]{1,0:T(8,128)(2,1)S(1)}, u32[]{:S(2)}, u32[]{:S(2)}) collective-permute-start(bf16[96,128]{1,0:T(8,128)(2,1)S(1)} %pack.1), channel_id=1, source_target_pairs={{0,256},{256,0},{1,257},{257,1},{2,258},{258,2},{3,259},{259,3},{4... | collective-permute-start | bytes 73736 | tf_op jit(solution)/shard_map/ppermute | solution.py:227
  24.1 3.2 %collective-permute-done = bf16[96,128]{1,0:T(8,128)(2,1)S(1)} collective-permute-done((bf16[96,128]{1,0:T(8,128)(2,1)S(1)}, bf16[96,128]{1,0:T(8,128)(2,1)S(1)}, u32[]{:S(2)}, u32[]{:S(2)}) %collective-permute-start) | collective-permute-done | bytes 24608 | tf_op jit(solution)/shard_map/ppermute | solution.py:227
  27.3 0.1 broadcast_in_dim.2
  27.5 14.8 %all_to_all.10.refs_0_ = bf16[16,2,96,128]{3,2,1,0:T(8,128)(2,1)S(1)} all-to-all(bf16[16,2,96,128]{3,2,1,0:T(8,128)(2,1)S(1)} %broadcast_in_dim.2), channel_id=1, replica_groups={{160,0,16,32,48,64,80,96,112,128,144,176,192,208,224,240},{161,1,17,33,..., dimensions={0} | all-to-all | bytes 1572864 | tf_op jit(solution)/shard_map/all_to_all | solution.py:242
  42.3 0.0 collective-permute-done.1.refs_2_
  42.3 0.0 copy-done.2
  42.3 0.0 copy-done.3
  42.3 0.0 copy-done.4
  42.3 0.0 copy-done.5
  42.3 0.0 copy-done.6
  42.3 0.0 copy-done.7
  42.3 2.5 %terms.1 = (bf16[16,12,120]{2,1,0:T(8,128)(2,1)S(1)}, f32[12,120]{1,0:T(8,128)S(1)}) custom-call(bf16[16,2,96,128]{3,2,1,0:T(8,128)(2,1)S(1)} %all_to_all.10.refs_0_, bf16[4,128,3840]{2,1,0:T(8,128)(2,1)S(1)} %hold.1.refs_1_, bf16[4,128,3840]{2,1,0:T(8,128)(2,1)S(1)} %collective-permute-done.1.refs_2_, bf16[4,96,120]{2,1,0:T(8,128)(2,1)S(1)} %bitcast.8, ...), custom_call_target="tpu_custom_call" | custom-call | flops 707788800 | bytes 8388608 | tf_op jit(solution)/shard_map/terms/pallas_call | solution.py:245
  44.8 18.1 %all_to_all.11.terms_ref = bf16[16,12,120]{2,1,0:T(8,128)(2,1)S(1)} all-to-all(bf16[16,12,120]{2,1,0:T(8,128)(2,1)S(1)} %get-tuple-element.7), channel_id=1, replica_groups={{7,9,6,8,5,11,4,10,3,13,2,12,1,15,0,14},{23,25,22,24,21,27,20,26,19,29,..., dimensions={0} | all-to-all | bytes 92160 | tf_op jit(solution)/shard_map/all_to_all | solution.py:269
  63.0 0.6 finish.1
  (1 shorter events, 0.0 us)
Async XLA Ops:
  0.0 2.0 %copy-start = (bf16[4,120,3840]{2,1,0:T(8,128)(2,1)S(1)}, bf16[4,120,3840]{2,1,0:T(8,128)(2,1)}, u32[]{:S(2)}) copy-start(bf16[4,120,3840]{2,1,0:T(8,128)(2,1)} %vv_hbm.1) | copy-start | bytes 11059204
  2.0 0.9 %copy-start.1 = (bf16[4,96,96]{2,1,0:T(8,128)(2,1)S(1)}, bf16[4,96,96]{2,1,0:T(8,128)(2,1)}, u32[]{:S(2)}) copy-start(bf16[4,96,96]{2,1,0:T(8,128)(2,1)} %screened_ref.1) | copy-start | bytes 221188
  3.9 38.4 %collective-permute-start.1 = (bf16[4,128,3840]{2,1,0:T(8,128)(2,1)S(1)}, bf16[4,128,3840]{2,1,0:T(8,128)(2,1)S(1)}, u32[]{:S(2)}, u32[]{:S(2)}) collective-permute-start(bf16[4,128,3840]{2,1,0:T(8,128)(2,1)S(1)} %hold.1.refs_1_), channel_id=1, source_target_pairs={{0,1},{1,0},{2,3},{3,2},{4,5},{5,4},{6,7},{7,6},{8,9},{9,8},{10,11... | collective-permute-start | bytes 11796488 | tf_op jit(solution)/shard_map/ppermute | solution.py:239
  12.7 29.6 %copy-start.2 = (bf16[4,120,96]{1,2,0:T(8,128)(2,1)S(1)}, bf16[4,120,96]{1,2,0:T(8,128)(2,1)}, u32[]{:S(2)}) copy-start(bf16[4,120,96]{1,2,0:T(8,128)(2,1)} %param.11) | copy-start | bytes 276484
  12.7 29.6 %copy-start.3 = (bf16[192,120]{1,0:T(8,128)(2,1)S(1)}, bf16[192,120]{1,0:T(8,128)(2,1)}, u32[]{:S(2)}) copy-start(bf16[192,120]{1,0:T(8,128)(2,1)} %refs_4_.1) | copy-start | bytes 138244
  12.7 29.6 %copy-start.4 = (f32[3840]{0:T(1024)S(1)}, f32[3840]{0:T(1024)}, u32[]{:S(2)}) copy-start(f32[3840]{0:T(1024)} %param.13) | copy-start | bytes 46084
  12.7 29.6 %copy-start.5 = (f32[96]{0:T(128)S(1)}, f32[96]{0:T(128)}, u32[]{:S(2)}) copy-start(f32[96]{0:T(128)} %param.12) | copy-start | bytes 1156
  12.7 29.6 %copy-start.6 = (s32[96]{0:T(128)S(1)}, s32[96]{0:T(128)}, u32[]{:S(2)}) copy-start(s32[96]{0:T(128)} %param.14) | copy-start | bytes 1156
  12.7 29.6 %copy-start.7 = (s32[120]{0:T(128)S(1)}, s32[120]{0:T(128)}, u32[]{:S(2)}) copy-start(s32[120]{0:T(128)} %param.15) | copy-start | bytes 1444
  14.0 13.3 %collective-permute-start = (bf16[96,128]{1,0:T(8,128)(2,1)S(1)}, bf16[96,128]{1,0:T(8,128)(2,1)S(1)}, u32[]{:S(2)}, u32[]{:S(2)}) collective-permute-start(bf16[96,128]{1,0:T(8,128)(2,1)S(1)} %pack.1), channel_id=1, source_target_pairs={{0,256},{256,0},{1,257},{257,1},{2,258},{258,2},{3,259},{259,3},{4... | collective-permute-start | bytes 73736 | tf_op jit(solution)/shard_map/ppermute | solution.py:227

commit v3 on v2

--- a/solution.py
+++ b/solution.py
@@ -39,11 +39,12 @@
     for k in range(0, chips, 2):
         pair = middle[k : k + 2]
         listed += [2 * a + 1 for a in pair] + [2 * a for a in pair]
-    return listed
+    first = count // 2 + 1
+    return [first, *(place for place in listed if place != first)]
 
 
 def plane_order(count):
-    first = 2 * count // 3
+    first = count // 3
     return [first, *(place for place in range(count) if place != first)]
 
 

time: 63.9 us -> 64.5 us (level)
  blocking collectives: 32.9 us -> 33.6 us
    all_to_all x1, blocking collectives: 14.8 us -> 17.8 us  [on_device(): lax.all_to_all(both, PLANE, 0, 0, tiled=True, axis_index_groups=[plane])]
    all_to_all x1, blocking collectives: 18.1 us -> 15.8 us  [on_device(): lax.all_to_all(terms, WINDOW, 0, 0, tiled=True, axis_index_groups=[window])]
where the time goes in v3:
time: 64.5 us; the launch traced here: 64.2 us
  blocking collectives  33.6 us (52%)
  starting transfers between devices  18.8 us (29%)
  Pallas kernels  5.39 us (8%)
  waiting for transfers between devices  3.18 us (5%)
  local copies, waits for them, and re-layouts  3.12 us (5%)
    all_to_all x1, blocking collectives, on_device(): lax.all_to_all(both, PLANE, 0, 0, tiled=True, axis_index_groups=[plane])  17.8 us
    all_to_all x1, blocking collectives, on_device(): lax.all_to_all(terms, WINDOW, 0, 0, tiled=True, axis_index_groups=[window])  15.8 us
    ppermute x1, starting transfers between devices, on_device(): far = lax.ppermute(block, 'half', cores)  10.1 us
    ppermute x1, starting transfers between devices, on_device(): joint_peer = lax.ppermute(joint, 'grp', cores)  8.75 us
    ppermute x1, waiting for transfers between devices, on_device(): far = lax.ppermute(block, 'half', cores)  3.18 us
    unnamed x16, local copies, waits for them, and re-layouts  2.97 us
    pallas_call x1, Pallas kernels, on_device(): pl.pallas_call(lambda *refs: term_kernel(plane, window, *refs), out_shape...  2.51 us
    pallas_call x1, Pallas kernels, on_device(): pl.pallas_call(pack_kernel, out_shape=jax.ShapeDtypeStruct((occupied, LAN...  1.29 us
  transfers between devices with their start and end apart: 2, of which 1 were waited for; matrix products, arithmetic and copies ran while one was open for 0% of the time, Pallas kernels for 2%

profile of v3, /device:TPU:1, one launch (start us, length us, event | category | flops | bytes accessed | tf_op | source)
XLA Modules:
  0.0 64.2 jit_solution(18090553636713477750)
XLA Ops:
  0.0 0.0 copy-start
  0.0 2.0 %copy-done = bf16[4,120,3840]{2,1,0:T(8,128)(2,1)S(1)} copy-done((bf16[4,120,3840]{2,1,0:T(8,128)(2,1)S(1)}, bf16[4,120,3840]{2,1,0:T(8,128)(2,1)}, u32[]{:S(2)}) %copy-start) | copy-done | bytes 3686424
  2.0 0.0 copy-start.1
  2.0 0.9 %copy-done.1 = bf16[4,96,96]{2,1,0:T(8,128)(2,1)S(1)} copy-done((bf16[4,96,96]{2,1,0:T(8,128)(2,1)S(1)}, bf16[4,96,96]{2,1,0:T(8,128)(2,1)}, u32[]{:S(2)}) %copy-start.1) | copy-done | bytes 73752
  2.9 1.0 %hold.1.refs_1_ = bf16[4,128,3840]{2,1,0:T(8,128)(2,1)S(1)} custom-call(bf16[4,120,3840]{2,1,0:T(8,128)(2,1)S(1)} %copy-done, bf16[4,96,96]{2,1,0:T(8,128)(2,1)S(1)} %copy-done.1), custom_call_target="tpu_custom_call" | custom-call | flops 100000000 | bytes 8388608 | tf_op jit(solution)/shard_map/hold/pallas_call | solution.py:230
  3.9 8.7 %collective-permute-start.1 = (bf16[4,128,3840]{2,1,0:T(8,128)(2,1)S(1)}, bf16[4,128,3840]{2,1,0:T(8,128)(2,1)S(1)}, u32[]{:S(2)}, u32[]{:S(2)}) collective-permute-start(bf16[4,128,3840]{2,1,0:T(8,128)(2,1)S(1)} %hold.1.refs_1_), channel_id=1, source_target_pairs={{0,1},{1,0},{2,3},{3,2},{4,5},{5,4},{6,7},{7,6},{8,9},{9,8},{10,11... | collective-permute-start | bytes 11796488 | tf_op jit(solution)/shard_map/ppermute | solution.py:240
  12.7 0.0 copy-start.2
  12.7 0.0 copy-start.3
  12.7 0.0 copy-start.4
  12.7 0.0 copy-start.5
  12.7 0.0 copy-start.6
  12.7 0.0 copy-start.7
  12.7 1.3 %pack.1 = bf16[96,128]{1,0:T(8,128)(2,1)S(1)} custom-call(bf16[192,120]{1,0:T(8,128)(2,1)} %refs_4_.1, bf16[4,96,120]{2,1,0:T(8,128)(2,1)} %bitcast.7), custom_call_target="tpu_custom_call" | custom-call | flops 20000000000 | bytes 1000000 | tf_op jit(solution)/shard_map/pack/pallas_call | solution.py:213
  14.0 10.1 %collective-permute-start = (bf16[96,128]{1,0:T(8,128)(2,1)S(1)}, bf16[96,128]{1,0:T(8,128)(2,1)S(1)}, u32[]{:S(2)}, u32[]{:S(2)}) collective-permute-start(bf16[96,128]{1,0:T(8,128)(2,1)S(1)} %pack.1), channel_id=1, source_target_pairs={{0,256},{256,0},{1,257},{257,1},{2,258},{258,2},{3,259},{259,3},{4... | collective-permute-start | bytes 73736 | tf_op jit(solution)/shard_map/ppermute | solution.py:228
  24.1 3.2 %collective-permute-done = bf16[96,128]{1,0:T(8,128)(2,1)S(1)} collective-permute-done((bf16[96,128]{1,0:T(8,128)(2,1)S(1)}, bf16[96,128]{1,0:T(8,128)(2,1)S(1)}, u32[]{:S(2)}, u32[]{:S(2)}) %collective-permute-start) | collective-permute-done | bytes 24608 | tf_op jit(solution)/shard_map/ppermute | solution.py:228
  27.3 0.1 broadcast_in_dim.2
  27.5 17.8 %all_to_all.10.refs_0_ = bf16[16,2,96,128]{3,2,1,0:T(8,128)(2,1)S(1)} all-to-all(bf16[16,2,96,128]{3,2,1,0:T(8,128)(2,1)S(1)} %broadcast_in_dim.2), channel_id=1, replica_groups={{80,0,16,32,48,64,96,112,128,144,160,176,192,208,224,240},{81,1,17,33,4..., dimensions={0} | all-to-all | bytes 1572864 | tf_op jit(solution)/shard_map/all_to_all | solution.py:243
  45.3 0.0 collective-permute-done.1.refs_2_
  45.3 0.0 copy-done.2
  45.3 0.0 copy-done.3
  45.3 0.0 copy-done.4
  45.3 0.0 copy-done.5
  45.3 0.0 copy-done.6
  45.3 0.0 copy-done.7
  45.3 2.5 %terms.1 = (bf16[16,12,120]{2,1,0:T(8,128)(2,1)S(1)}, f32[12,120]{1,0:T(8,128)S(1)}) custom-call(bf16[16,2,96,128]{3,2,1,0:T(8,128)(2,1)S(1)} %all_to_all.10.refs_0_, bf16[4,128,3840]{2,1,0:T(8,128)(2,1)S(1)} %hold.1.refs_1_, bf16[4,128,3840]{2,1,0:T(8,128)(2,1)S(1)} %collective-permute-done.1.refs_2_, bf16[4,96,120]{2,1,0:T(8,128)(2,1)S(1)} %bitcast.8, ...), custom_call_target="tpu_custom_call" | custom-call | flops 707788800 | bytes 8388608 | tf_op jit(solution)/shard_map/terms/pallas_call | solution.py:246
  47.8 15.8 %all_to_all.11.terms_ref = bf16[16,12,120]{2,1,0:T(8,128)(2,1)S(1)} all-to-all(bf16[16,12,120]{2,1,0:T(8,128)(2,1)S(1)} %get-tuple-element.7), channel_id=1, replica_groups={{9,7,6,8,5,11,4,10,3,13,2,12,1,15,0,14},{25,23,22,24,21,27,20,26,19,29,..., dimensions={0} | all-to-all | bytes 92160 | tf_op jit(solution)/shard_map/all_to_all | solution.py:270
  63.6 0.6 finish.1
  (1 shorter events, 0.0 us)
Async XLA Ops:
  0.0 2.0 %copy-start = (bf16[4,120,3840]{2,1,0:T(8,128)(2,1)S(1)}, bf16[4,120,3840]{2,1,0:T(8,128)(2,1)}, u32[]{:S(2)}) copy-start(bf16[4,120,3840]{2,1,0:T(8,128)(2,1)} %vv_hbm.1) | copy-start | bytes 11059204
  2.0 0.9 %copy-start.1 = (bf16[4,96,96]{2,1,0:T(8,128)(2,1)S(1)}, bf16[4,96,96]{2,1,0:T(8,128)(2,1)}, u32[]{:S(2)}) copy-start(bf16[4,96,96]{2,1,0:T(8,128)(2,1)} %screened_ref.1) | copy-start | bytes 221188
  3.9 41.4 %collective-permute-start.1 = (bf16[4,128,3840]{2,1,0:T(8,128)(2,1)S(1)}, bf16[4,128,3840]{2,1,0:T(8,128)(2,1)S(1)}, u32[]{:S(2)}, u32[]{:S(2)}) collective-permute-start(bf16[4,128,3840]{2,1,0:T(8,128)(2,1)S(1)} %hold.1.refs_1_), channel_id=1, source_target_pairs={{0,1},{1,0},{2,3},{3,2},{4,5},{5,4},{6,7},{7,6},{8,9},{9,8},{10,11... | collective-permute-start | bytes 11796488 | tf_op jit(solution)/shard_map/ppermute | solution.py:240
  12.7 32.6 %copy-start.2 = (bf16[4,120,96]{1,2,0:T(8,128)(2,1)S(1)}, bf16[4,120,96]{1,2,0:T(8,128)(2,1)}, u32[]{:S(2)}) copy-start(bf16[4,120,96]{1,2,0:T(8,128)(2,1)} %param.11) | copy-start | bytes 276484
  12.7 32.6 %copy-start.3 = (bf16[192,120]{1,0:T(8,128)(2,1)S(1)}, bf16[192,120]{1,0:T(8,128)(2,1)}, u32[]{:S(2)}) copy-start(bf16[192,120]{1,0:T(8,128)(2,1)} %refs_4_.1) | copy-start | bytes 138244
  12.7 32.6 %copy-start.4 = (f32[3840]{0:T(1024)S(1)}, f32[3840]{0:T(1024)}, u32[]{:S(2)}) copy-start(f32[3840]{0:T(1024)} %param.13) | copy-start | bytes 46084
  12.7 32.6 %copy-start.5 = (f32[96]{0:T(128)S(1)}, f32[96]{0:T(128)}, u32[]{:S(2)}) copy-start(f32[96]{0:T(128)} %param.12) | copy-start | bytes 1156
  12.7 32.6 %copy-start.6 = (s32[96]{0:T(128)S(1)}, s32[96]{0:T(128)}, u32[]{:S(2)}) copy-start(s32[96]{0:T(128)} %param.14) | copy-start | bytes 1156
  12.7 32.6 %copy-start.7 = (s32[120]{0:T(128)S(1)}, s32[120]{0:T(128)}, u32[]{:S(2)}) copy-start(s32[120]{0:T(128)} %param.15) | copy-start | bytes 1444
  14.0 13.3 %collective-permute-start = (bf16[96,128]{1,0:T(8,128)(2,1)S(1)}, bf16[96,128]{1,0:T(8,128)(2,1)S(1)}, u32[]{:S(2)}, u32[]{:S(2)}) collective-permute-start(bf16[96,128]{1,0:T(8,128)(2,1)S(1)} %pack.1), channel_id=1, source_target_pairs={{0,256},{256,0},{1,257},{257,1},{2,258},{258,2},{3,259},{259,3},{4... | collective-permute-start | bytes 73736 | tf_op jit(solution)/shard_map/ppermute | solution.py:228
